TPU v7x, 32 devices: a whole 2x2x4 slice. The times are simulated.
32 devices in a mesh: dp: 4 (over y, x), row: 2 (over core), col: 4 (over z).
Axes of the slice: x: 2, y: 2, z: 4, core: 2. Of those that a mesh axis runs over, the one named last changes fastest.
Arguments:
- tokens: bfloat16 [4096, 2048], P('dp', ('row', 'col')), may hold values from -40 to 40
- gain_attn: float32 [2048], P(('row', 'col')), may hold values from 0.5 to 1.5
- gain_ffn: float32 [2048], P(('row', 'col')), may hold values from 0.5 to 1.5
- w_query: bfloat16 [2048, 2048], P('row', 'col'), may hold values from -0.125 to 0.125
- w_key: bfloat16 [2048, 2048], P('row', 'col'), may hold values from -0.125 to 0.125
- w_value: bfloat16 [2048, 2048], P('row', 'col'), may hold values from -0.125 to 0.125
- w_out: bfloat16 [2048, 2048], P('col', 'row'), may hold values from -1 to 1
- w_gate: bfloat16 [2048, 8192], P('row', 'col'), may hold values from -0.125 to 0.125
- w_up: bfloat16 [2048, 8192], P('row', 'col'), may hold values from -0.125 to 0.125
- w_down: bfloat16 [8192, 2048], P('col', 'row'), may hold values from -0.0625 to 0.0625
- grad_output: bfloat16 [4096, 2048], P('dp', ('row', 'col')), may hold values from -6 to 6
- segments: int32 [4, 1024], P('dp'), may hold values from 0 to 2, as said below
- positions: int32 [4, 1024], P('dp'), may hold values from 0 to 2047, as said below
Outputs:
- output: float32 [4096, 2048], P('dp', ('row', 'col'))
- grad_tokens: float32 [4096, 2048], P('dp', ('row', 'col'))
- grad_gain_attn: float32 [8, 4, 64], P(('row', 'col'), 'dp')
- grad_gain_ffn: float32 [8, 4, 64], P(('row', 'col'), 'dp')
- grad_w_query: float32 [2, 4, 256, 2048], P('row', 'dp', None, 'col')
- grad_w_key: float32 [2, 4, 256, 2048], P('row', 'dp', None, 'col')
- grad_w_value: float32 [2, 4, 256, 2048], P('row', 'dp', None, 'col')
- grad_w_out: float32 [4, 4, 128, 2048], P('col', 'dp', None, 'row')
- grad_w_gate: float32 [2, 4, 256, 8192], P('row', 'dp', None, 'col')
- grad_w_up: float32 [2, 4, 256, 8192], P('row', 'dp', None, 'col')
- grad_w_down: float32 [4, 4, 512, 2048], P('col', 'dp', None, 'row')
Inputs may be any that keep to these rules, and one draw needn't show every extreme that they name: `segments`: within a sequence the numbers never fall; each sequence holds three documents. `positions`: positions count up by one inside a document; the first document of a sequence starts at a position no larger than 2048 minus its length, the others at 0.
All inputs are finite; a program needn't handle non-finite values.
Results may differ from a plain program's by a relative error of at most 0.015.
Values may be sent and summed in bfloat16 or wider, within the bound.
A program may use at most 256 MiB of HBM per device.

v0:
```python
import jax
import jax.numpy as jnp
from jax import lax
from jax.sharding import PartitionSpec as P

D = 2048
HD = 64
norm_eps = 1e-05
rope_base = 130000.0
masked_score = -1e30


def width_total(partial_sums):
    return lax.psum(partial_sums, ("row", "col"))


def gather_cols(pieces):
    return lax.all_gather(pieces, "col", axis=1, tiled=True)


def sum_cols(partial_sums):
    return lax.psum_scatter(partial_sums, "col", scatter_dimension=1, tiled=True)


def gather_rows(pieces):
    return lax.all_gather(pieces, "row", axis=2, tiled=True)


def sum_rows(partial_sums):
    return lax.psum_scatter(partial_sums, "row", scatter_dimension=2, tiled=True)


def product(left, right):
    return jnp.dot(left, right, preferred_element_type=jnp.float32)


def contract_rows(left, right):
    return jnp.einsum("ta,tb->ab", left, right, preferred_element_type=jnp.float32)


def times_transposed(left, right):
    return jnp.einsum("ta,ba->tb", left, right, preferred_element_type=jnp.float32)


def norm_forward(residual, gain_vec):
    squares = width_total(jnp.sum(residual * residual, axis=1))
    scale_inv = lax.rsqrt(squares / D + norm_eps)
    normed = residual * scale_inv[:, None]
    return (normed, scale_inv, (normed * gain_vec).astype(jnp.bfloat16))


def norm_backward(grad_normed_out, normed, scale_inv, gain_vec):
    grad_normed = grad_normed_out * gain_vec
    inner_sum = width_total(jnp.sum(grad_normed * normed, axis=1))
    grad_input = scale_inv[:, None] * (grad_normed - normed * (inner_sum / D)[:, None])
    return (grad_input, jnp.sum(grad_normed_out * normed, axis=0))


def rope_tables(positions):
    half_steps = jnp.arange(HD // 2, dtype=jnp.float32)
    inv_freq = rope_base ** (-2.0 * half_steps / HD)
    angles = positions.astype(jnp.float32)[:, None] * inv_freq[None, :]
    return (jnp.cos(angles)[:, None, :], jnp.sin(angles)[:, None, :])


def rotate(values, cos_table, sin_table):
    half_dim = values.shape[-1] // 2
    first_half = values[..., :half_dim]
    second_half = values[..., half_dim:]
    return jnp.concatenate(
        [
            first_half * cos_table - second_half * sin_table,
            second_half * cos_table + first_half * sin_table,
        ],
        axis=-1,
    )


def unrotate(values, cos_table, sin_table):
    half_dim = values.shape[-1] // 2
    first_half = values[..., :half_dim]
    second_half = values[..., half_dim:]
    return jnp.concatenate(
        [
            first_half * cos_table + second_half * sin_table,
            second_half * cos_table - first_half * sin_table,
        ],
        axis=-1,
    )


def score_rows(query_part, key_rows, segment, row_start):
    row_count = query_part.shape[0]
    seq_len = key_rows.shape[0]
    scores = jnp.einsum(
        "qhd,khd->hqk", query_part, key_rows, preferred_element_type=jnp.float32
    ) * key_rows.shape[2] ** (-0.5)
    query_slot = row_start + jnp.arange(row_count)
    key_slot = jnp.arange(seq_len)
    query_seg = segment[row_start : row_start + row_count]
    allowed = (key_slot[None, :] <= query_slot[:, None]) & (query_seg[:, None] == segment[None, :])
    return jnp.where(allowed[None], scores, masked_score)


def attend_forward(inputs):
    queries, key_rows, value_rows, segment = inputs
    seq_len = queries.shape[0]
    span = min(512, seq_len)
    results = []
    log_parts = []
    for row_start in range(0, seq_len, span):
        scores = score_rows(queries[row_start : row_start + span], key_rows, segment, row_start)
        log_total = jnp.log(jnp.sum(jnp.exp(scores), axis=-1))
        attn_probs = jnp.exp(scores - log_total[..., None]).astype(jnp.bfloat16)
        results.append(
            jnp.einsum("hqk,khd->qhd", attn_probs, value_rows, preferred_element_type=jnp.float32)
        )
        log_parts.append(log_total)
    return (jnp.concatenate(results, axis=0), jnp.concatenate(log_parts, axis=1))


def attend_backward(inputs):
    queries, key_rows, value_rows, segment, log_totals, grad_rows = inputs
    seq_len = queries.shape[0]
    span = min(512, seq_len)
    score_scale = queries.shape[2] ** (-0.5)
    grad_query_parts = []
    grad_keys = jnp.zeros(key_rows.shape, jnp.float32)
    grad_values = jnp.zeros(value_rows.shape, jnp.float32)
    for row_start in range(0, seq_len, span):
        query_part = queries[row_start : row_start + span]
        grad_part = grad_rows[row_start : row_start + span]
        scores = score_rows(query_part, key_rows, segment, row_start)
        attn_probs = jnp.exp(scores - log_totals[:, row_start : row_start + span, None])
        grad_probs = jnp.einsum(
            "qhd,khd->hqk", grad_part, value_rows, preferred_element_type=jnp.float32
        )
        weighted = jnp.sum(attn_probs * grad_probs, axis=-1, keepdims=True)
        grad_scores = (attn_probs * (grad_probs - weighted) * score_scale).astype(jnp.bfloat16)
        grad_query_parts.append(
            jnp.einsum("hqk,khd->qhd", grad_scores, key_rows, preferred_element_type=jnp.float32)
        )
        grad_keys = grad_keys + jnp.einsum(
            "hqk,qhd->khd", grad_scores, query_part, preferred_element_type=jnp.float32
        )
        grad_values = grad_values + jnp.einsum(
            "hqk,qhd->khd",
            attn_probs.astype(jnp.bfloat16),
            grad_part,
            preferred_element_type=jnp.float32,
        )
    return (jnp.concatenate(grad_query_parts, axis=0), grad_keys, grad_values)


def as_blocks(matrix):
    return matrix.reshape((1, 1) + matrix.shape)


def body(
    tokens,
    gain_attn,
    gain_ffn,
    w_query,
    w_key,
    w_value,
    w_out,
    w_gate,
    w_up,
    w_down,
    grad_output,
    segments,
    positions,
):
    residual = tokens.astype(jnp.float32)
    tok_count = residual.shape[0]
    seq_count, seq_len = segments.shape
    cos_table, sin_table = rope_tables(positions.reshape(tok_count))
    normed_one, inv_one, hidden_one = norm_forward(residual, gain_attn)
    gathered_one = gather_cols(hidden_one)
    projected = jnp.stack(
        [
            product(gathered_one, w_query),
            product(gathered_one, w_key),
            product(gathered_one, w_value),
        ]
    )
    local_qkv = sum_rows(projected)
    head_shape = (seq_count, seq_len, local_qkv.shape[2] // HD, HD)
    flat_heads = (tok_count, local_qkv.shape[2] // HD, HD)
    queries = (
        rotate(local_qkv[0].reshape(flat_heads), cos_table, sin_table)
        .astype(jnp.bfloat16)
        .reshape(head_shape)
    )
    key_rows = (
        rotate(local_qkv[1].reshape(flat_heads), cos_table, sin_table)
        .astype(jnp.bfloat16)
        .reshape(head_shape)
    )
    value_rows = local_qkv[2].astype(jnp.bfloat16).reshape(head_shape)
    attended, log_totals = lax.map(attend_forward, (queries, key_rows, value_rows, segments))
    heads_out = attended.reshape(tok_count, -1).astype(jnp.bfloat16)
    heads_all = gather_rows(heads_out[None])[0]
    middle = residual + sum_cols(product(heads_all, w_out))
    normed_two, inv_two, hidden_two = norm_forward(middle, gain_ffn)
    gathered_two = gather_cols(hidden_two)
    gate_up = sum_rows(jnp.stack([product(gathered_two, w_gate), product(gathered_two, w_up)]))
    gate_pre = gate_up[0]
    up_pre = gate_up[1]
    gate_sigmoid = jax.nn.sigmoid(gate_pre)
    hidden_units = (gate_pre * gate_sigmoid * up_pre).astype(jnp.bfloat16)
    units_all = gather_rows(hidden_units[None])[0]
    output = middle + sum_cols(product(units_all, w_down))
    grad_all = gather_cols(grad_output)
    units_all = gather_rows(hidden_units[None])[0]
    grad_w_down = contract_rows(units_all, grad_all)
    grad_units = sum_rows(times_transposed(grad_all, w_down)[None])[0]
    grad_gate = (
        grad_units * up_pre * gate_sigmoid * (1.0 + gate_pre * (1.0 - gate_sigmoid))
    ).astype(jnp.bfloat16)
    grad_up = (grad_units * gate_pre * gate_sigmoid).astype(jnp.bfloat16)
    gathered_two = gather_cols(hidden_two)
    grad_pair = gather_rows(jnp.stack([grad_gate, grad_up]))
    grad_w_gate = contract_rows(gathered_two, grad_pair[0])
    grad_w_up = contract_rows(gathered_two, grad_pair[1])
    grad_two = sum_cols(
        times_transposed(grad_pair[0], w_gate) + times_transposed(grad_pair[1], w_up)
    )
    grad_norm_two, grad_gain_ffn = norm_backward(grad_two, normed_two, inv_two, gain_ffn)
    grad_middle = grad_output.astype(jnp.float32) + grad_norm_two
    grad_branch = gather_cols(grad_middle.astype(jnp.bfloat16))
    heads_all = gather_rows(heads_out[None])[0]
    grad_w_out = contract_rows(heads_all, grad_branch)
    grad_heads = sum_rows(times_transposed(grad_branch, w_out)[None])[0].astype(jnp.bfloat16)
    grad_queries, grad_keys, grad_values = lax.map(
        attend_backward,
        (queries, key_rows, value_rows, segments, log_totals, grad_heads.reshape(head_shape)),
    )
    grad_query_pre = (
        unrotate(grad_queries.reshape(flat_heads), cos_table, sin_table)
        .reshape(tok_count, -1)
        .astype(jnp.bfloat16)
    )
    grad_key_pre = (
        unrotate(grad_keys.reshape(flat_heads), cos_table, sin_table)
        .reshape(tok_count, -1)
        .astype(jnp.bfloat16)
    )
    grad_value_pre = grad_values.reshape(tok_count, -1).astype(jnp.bfloat16)
    grad_triple = gather_rows(jnp.stack([grad_query_pre, grad_key_pre, grad_value_pre]))
    gathered_one = gather_cols(hidden_one)
    grad_w_query = contract_rows(gathered_one, grad_triple[0])
    grad_w_key = contract_rows(gathered_one, grad_triple[1])
    grad_w_value = contract_rows(gathered_one, grad_triple[2])
    grad_one = sum_cols(
        times_transposed(grad_triple[0], w_query)
        + times_transposed(grad_triple[1], w_key)
        + times_transposed(grad_triple[2], w_value)
    )
    grad_norm_one, grad_gain_attn = norm_backward(grad_one, normed_one, inv_one, gain_attn)
    grad_tokens = grad_middle + grad_norm_one
    reduced = (
        lax.psum_scatter(grad_gain_attn, "dp", scatter_dimension=0, tiled=True),
        lax.psum_scatter(grad_gain_ffn, "dp", scatter_dimension=0, tiled=True),
        lax.psum_scatter(grad_w_query, "dp", scatter_dimension=0, tiled=True),
        lax.psum_scatter(grad_w_key, "dp", scatter_dimension=0, tiled=True),
        lax.psum_scatter(grad_w_value, "dp", scatter_dimension=0, tiled=True),
        lax.psum_scatter(grad_w_out, "dp", scatter_dimension=0, tiled=True),
        lax.psum_scatter(grad_w_gate, "dp", scatter_dimension=0, tiled=True),
        lax.psum_scatter(grad_w_up, "dp", scatter_dimension=0, tiled=True),
        lax.psum_scatter(grad_w_down, "dp", scatter_dimension=0, tiled=True),
    )
    gate_share, up_share = (reduced[6], reduced[7])
    return (
        output,
        grad_tokens,
        as_blocks(reduced[0]),
        as_blocks(reduced[1]),
        as_blocks(reduced[2]),
        as_blocks(reduced[3]),
        as_blocks(reduced[4]),
        as_blocks(reduced[5]),
        as_blocks(gate_share),
        as_blocks(up_share),
        as_blocks(reduced[8]),
    )


def solution(mesh):
    return jax.shard_map(
        body,
        mesh=mesh,
        in_specs=(
            P("dp", ("row", "col")),
            P(("row", "col")),
            P(("row", "col")),
            P("row", "col"),
            P("row", "col"),
            P("row", "col"),
            P("col", "row"),
            P("row", "col"),
            P("row", "col"),
            P("col", "row"),
            P("dp", ("row", "col")),
            P("dp", None),
            P("dp", None),
        ),
        out_specs=(
            P("dp", ("row", "col")),
            P("dp", ("row", "col")),
            P(("row", "col"), "dp", None),
            P(("row", "col"), "dp", None),
            P("row", "dp", None, "col"),
            P("row", "dp", None, "col"),
            P("row", "dp", None, "col"),
            P("col", "dp", None, "row"),
            P("row", "dp", None, "col"),
            P("row", "dp", None, "col"),
            P("col", "dp", None, "row"),
        ),
        check_vma=False,
    )
```

profile of v0, /device:TPU:0, one launch (start us, length us, event | category | flops | bytes accessed | tf_op | source)
XLA Modules:
  0.0 1258.6 jit_solution(7421168657881235583)
XLA Ops:
  8.6 18.5 %psum.28 = f32[1024]{0:T(1024)S(1)} all-reduce(f32[1024]{0:T(1024)S(1)} %fusion.95), channel_id=1, replica_groups=mesh['dp'=4,'row'=2,'col'=4] {'row','col'}, use_global_device_ids=true, to_apply=%region_1.0 | all-reduce | flops 1024 | bytes 8192 | tf_op jit(solution)/shard_map/psum | solution.py:14
  29.3 44.6 %all-gather.9.cloned.1.call-done = bf16[1024,1024]{1,0:T(8,128)(2,1)} async-done(((bf16[1024,256]{1,0:T(8,128)(2,1)}), bf16[1024,1024]{1,0:T(8,128)(2,1)}) %all-gather.9.cloned.1.call-update) | async-done | bytes 2097168 | tf_op jit(solution)/shard_map/all_gather | solution.py:18
  128.6 10.4 all-gather.11.cloned.1.call-done
  144.1 77.5 %reduce-scatter.18.cloned.1.call-done = f32[1024,256]{1,0:T(8,128)} async-done(((f32[1024,1024]{1,0:T(8,128)}), f32[1024,256]{1,0:T(8,128)}) %reduce-scatter.18.cloned.1.call-update) | async-done | bytes 1048592 | tf_op jit(solution)/shard_map/reduce_scatter | solution.py:22
  223.1 16.6 %psum.29 = f32[1024]{0:T(1024)S(1)} all-reduce(f32[1024]{0:T(1024)S(1)} %get-tuple-element.68), channel_id=1, replica_groups=mesh['dp'=4,'row'=2,'col'=4] {'row','col'}, use_global_device_ids=true, to_apply=%region_7.8 | all-reduce | flops 1024 | bytes 8192 | tf_op jit(solution)/shard_map/psum | solution.py:14
  241.3 28.8 %all-gather.17.cloned.1.call-done = bf16[1024,1024]{1,0:T(8,128)(2,1)} async-done(((bf16[1024,256]{1,0:T(8,128)(2,1)}), bf16[1024,1024]{1,0:T(8,128)(2,1)}) %all-gather.17.cloned.1.call-update) | async-done | bytes 2097168 | tf_op jit(solution)/shard_map/all_gather | solution.py:18
  270.1 10.6 convolution_bitcast_fusion
  280.7 35.8 %all-gather.13.cloned.1.call-done = bf16[1024,1024]{1,0:T(8,128)(2,1)} async-done(((bf16[1024,256]{1,0:T(8,128)(2,1)}), bf16[1024,1024]{1,0:T(8,128)(2,1)}) %all-gather.13.cloned.1.call-update) | async-done | bytes 2097168 | tf_op jit(solution)/shard_map/all_gather | solution.py:18
  335.3 26.6 %reduce-scatter.20.cloned.1.call-done = f32[2,1024,1024]{2,1,0:T(8,128)} async-done(((f32[2,1024,2048]{2,1,0:T(8,128)}), f32[2,1024,1024]{2,1,0:T(8,128)}) %reduce-scatter.20.cloned.1.call-update) | async-done | bytes 8388624 | tf_op jit(solution)/shard_map/reduce_scatter | solution.py:30
  371.4 21.0 %all-gather.19.cloned.1.call-done = bf16[2,1024,2048]{2,1,0:T(8,128)(2,1)} async-done(((bf16[2,1024,1024]{2,1,0:T(8,128)(2,1)}), bf16[2,1024,2048]{2,1,0:T(8,128)(2,1)}) %all-gather.19.cloned.1.call-update) | async-done | bytes 8388624 | tf_op jit(solution)/shard_map/all_gather | solution.py:26
  406.6 78.1 %reduce-scatter.26.cloned.1.call-done = f32[1024,256]{1,0:T(8,128)} async-done(((f32[1024,1024]{1,0:T(8,128)}), f32[1024,256]{1,0:T(8,128)}) %reduce-scatter.26.cloned.1.call-update) | async-done | bytes 1048592 | tf_op jit(solution)/shard_map/reduce_scatter | solution.py:22
  486.3 16.0 %psum.30 = f32[1024]{0:T(1024)S(1)} all-reduce(f32[1024]{0:T(1024)S(1)} %get-tuple-element.53), channel_id=1, replica_groups=mesh['dp'=4,'row'=2,'col'=4] {'row','col'}, use_global_device_ids=true, to_apply=%region_13.14 | all-reduce | flops 1024 | bytes 8192 | tf_op jit(solution)/shard_map/psum | solution.py:14
  504.8 45.1 %all-gather.21.cloned.1.call-done = bf16[1024,1024]{1,0:T(8,128)(2,1)} async-done(((bf16[1024,256]{1,0:T(8,128)(2,1)}), bf16[1024,1024]{1,0:T(8,128)(2,1)}) %all-gather.21.cloned.1.call-update) | async-done | bytes 2097168 | tf_op jit(solution)/shard_map/all_gather | solution.py:18
  568.1 12.7 %fusion.29 = f32[4,64,1024]{2,1,0:T(8,128)} fusion(f32[4,512,1024]{2,1,0:T(8,128)} %fusion.5, f32[4,512,1024]{2,1,0:T(8,128)} %fusion.132, bf16[1024,4,32]{0,2,1:T(8,128)(2,1)S(1)} %copy-done.18, bf16[1024,4,32]{0,2,1:T(8,128)(2,1)S(1)} %copy-done.16), kind=kOutput, calls=%fused_computation.43 | convolution fusion | flops 279448576 | bytes 35127296 | tf_op jit(solution)/shard_map/while/body/eval_jaxpr/hqk,qhd->khd/dot_general | solution.py:143
  580.8 13.5 %fusion.74 = f32[512,4,64]{0,2,1:T(8,128)} fusion(f32[4,512,1024]{2,1,0:T(8,128)} %fusion.5, f32[4,512,1024]{2,1,0:T(8,128)} %fusion.132, bf16[1024,4,32]{0,2,1:T(8,128)(2,1)} %get-tuple-element.80, bf16[1024,4,32]{0,2,1:T(8,128)(2,1)S(1)} %copy-done.20), kind=kOutput, calls=%fused_computation.81 | convolution fusion | flops 279972864 | bytes 17825792 | tf_op jit(solution)/shard_map/while/body/eval_jaxpr/hqk,khd->qhd/dot_general | solution.py:141
  604.0 12.0 fusion.71
  616.0 14.0 %fusion.65 = f32[1024,4,64]{0,2,1:T(8,128)} fusion(f32[4,64,1024]{2,1,0:T(8,128)} %fusion.29, f32[4,512,1024]{2,1,0:T(8,128)} %fusion.4, f32[4,512,1024]{2,1,0:T(8,128)} %fusion.133, bf16[1024,4,32]{0,2,1:T(8,128)(2,1)} %get-tuple-element.89, bf16[1024,4,32]{0,2,1:T(8,128)(2,1)} %get-tuple-element.90), kind=kOutput, calls=%fused_computation.78 | convolution fusion | flops 279710720 | bytes 19398656 | tf_op jit(solution)/shard_map/while/body/eval_jaxpr/hqk,qhd->khd/dot_general | solution.py:143
  637.2 12.5 all-gather.23.cloned.1.call-done
  666.6 10.1 fusion.20
  676.8 10.7 fusion.18
  692.9 10.6 fusion.40
  703.6 10.7 fusion.42
  729.7 17.1 %reduce-scatter.30.cloned.1.call-done = f32[1024,256]{1,0:T(8,128)} async-done(((f32[1024,1024]{1,0:T(8,128)}), f32[1024,256]{1,0:T(8,128)}) %reduce-scatter.30.cloned.1.call-update) | async-done | bytes 1048592 | tf_op jit(solution)/shard_map/reduce_scatter | solution.py:22
  758.3 16.5 %psum.31 = f32[1024]{0:T(1024)S(1)} all-reduce(f32[1024]{0:T(1024)S(1)} %get-tuple-element.55), channel_id=1, replica_groups=mesh['dp'=4,'row'=2,'col'=4] {'row','col'}, use_global_device_ids=true, to_apply=%region_19.20 | all-reduce | flops 1024 | bytes 8192 | tf_op jit(solution)/shard_map/psum | solution.py:14
  776.0 50.8 %reduce-scatter.22.cloned.1.call-done = f32[1024,256]{1,0:T(8,128)} async-done(((f32[1024,1024]{1,0:T(8,128)}), f32[1024,256]{1,0:T(8,128)}) %reduce-scatter.22.cloned.1.call-update) | async-done | bytes 1048592 | tf_op jit(solution)/shard_map/reduce_scatter | solution.py:22
  830.0 87.1 %reduce-scatter.44.cloned.1.call-done = f32[512,1024]{1,0:T(8,128)} async-done(((f32[2048,1024]{1,0:T(8,128)}), f32[512,1024]{1,0:T(8,128)}) %reduce-scatter.44.cloned.1.call-update) | async-done | bytes 2097168 | tf_op jit(solution)/shard_map/reduce_scatter | solution.py:271
  917.1 38.6 %reduce-scatter.38.cloned.1.call-done = f32[128,1024]{1,0:T(8,128)} async-done(((f32[512,1024]{1,0:T(8,128)}), f32[128,1024]{1,0:T(8,128)}) %reduce-scatter.38.cloned.1.call-update) | async-done | bytes 524304 | tf_op jit(solution)/shard_map/reduce_scatter | solution.py:268
  955.7 90.0 %reduce-scatter.40.cloned.1.call-done = f32[256,2048]{1,0:T(8,128)} async-done(((f32[1024,2048]{1,0:T(8,128)}), f32[256,2048]{1,0:T(8,128)}) %reduce-scatter.40.cloned.1.call-update) | async-done | bytes 2097168 | tf_op jit(solution)/shard_map/reduce_scatter | solution.py:269
  1045.7 89.8 %reduce-scatter.42.cloned.1.call-done = f32[256,2048]{1,0:T(8,128)} async-done(((f32[1024,2048]{1,0:T(8,128)}), f32[256,2048]{1,0:T(8,128)}) %reduce-scatter.42.cloned.1.call-update) | async-done | bytes 2097168 | tf_op jit(solution)/shard_map/reduce_scatter | solution.py:270
  1135.6 38.8 %reduce-scatter.32.cloned.1.call-done = f32[256,512]{1,0:T(8,128)} async-done(((f32[1024,512]{1,0:T(8,128)}), f32[256,512]{1,0:T(8,128)}) %reduce-scatter.32.cloned.1.call-update) | async-done | bytes 524304 | tf_op jit(solution)/shard_map/reduce_scatter | solution.py:265
  1174.4 38.8 %reduce-scatter.34.cloned.1.call-done = f32[256,512]{1,0:T(8,128)} async-done(((f32[1024,512]{1,0:T(8,128)}), f32[256,512]{1,0:T(8,128)}) %reduce-scatter.34.cloned.1.call-update) | async-done | bytes 524304 | tf_op jit(solution)/shard_map/reduce_scatter | solution.py:266
  1213.1 38.8 %reduce-scatter.36.cloned.1.call-done = f32[256,512]{1,0:T(8,128)} async-done(((f32[1024,512]{1,0:T(8,128)}), f32[256,512]{1,0:T(8,128)}) %reduce-scatter.36.cloned.1.call-update) | async-done | bytes 524304 | tf_op jit(solution)/shard_map/reduce_scatter | solution.py:267
  (186 shorter events, 200.3 us)
Async XLA Ops:
  7.2 131.9 %copy-start = (bf16[512,1024]{1,0:T(8,128)(2,1)S(1)}, bf16[512,1024]{1,0:T(8,128)(2,1)}, u32[]{:S(2)}) copy-start(bf16[512,1024]{1,0:T(8,128)(2,1)} %param.19) | copy-start | bytes 3145732
  7.2 66.7 %all-gather.9.cloned.1.call-start = ((), (), s32[]{:S(2)}) async-start(), calls=%async_computation.15 | async-start | bytes 2621440 | tf_op jit(solution)/shard_map/all_gather | solution.py:18
  27.1 50.0 %copy-start.22 = (f32[1024]{0:T(1024)}, f32[1024]{0:T(1024)S(1)}, u32[]{:S(2)}) copy-start(f32[1024]{0:T(1024)S(1)} %add_rsqrt_fusion.1) | copy-start | bytes 12292
  29.2 47.9 %copy-start.34 = (bf16[1024,512]{1,0:T(8,128)(2,1)S(1)}, bf16[1024,512]{1,0:T(8,128)(2,1)}, u32[]{:S(2)}) copy-start(bf16[1024,512]{1,0:T(8,128)(2,1)} %param.17) | copy-start | bytes 3145732
  29.2 66.0 %reduce-scatter.16.cloned.1.call-start = ((), (), s32[]{:S(2)}) async-start(), calls=%async_computation.16 | async-start | bytes 9437184 | tf_op jit(solution)/shard_map/reduce_scatter | solution.py:30
  83.1 56.0 %all-gather.11.cloned.1.call-start = ((), (), s32[]{:S(2)}) async-start(), calls=%async_computation.17 | async-start | bytes 1572864 | tf_op jit(solution)/shard_map/all_gather | solution.py:26
  128.6 93.1 %reduce-scatter.18.cloned.1.call-start = ((), (), s32[]{:S(2)}) async-start(), calls=%async_computation.18 | async-start | bytes 5242880 | tf_op jit(solution)/shard_map/reduce_scatter | solution.py:22
  143.5 78.2 %copy-start.3 = (bf16[1024,256]{1,0:T(8,128)(2,1)S(1)}, bf16[1024,256]{1,0:T(8,128)(2,1)}, u32[]{:S(2)}) copy-start(bf16[1024,256]{1,0:T(8,128)(2,1)} %param.13) | copy-start | bytes 1572868
  143.5 96.2 %copy-start.24 = (f32[256]{0:T(256)S(1)}, f32[256]{0:T(256)}, u32[]{:S(2)}) copy-start(f32[256]{0:T(256)} %param.15) | copy-start | bytes 3076
  143.5 126.6 %all-gather.17.cloned.1.call-start = ((), (), s32[]{:S(2)}) async-start(), calls=%async_computation.23 | async-start | bytes 2621440 | tf_op jit(solution)/shard_map/all_gather | solution.py:18
  144.1 172.4 %all-gather.13.cloned.1.call-start = ((), (), s32[]{:S(2)}) async-start(), calls=%async_computation.19 | async-start | bytes 2621440 | tf_op jit(solution)/shard_map/all_gather | solution.py:18
  240.7 94.6 %reduce-scatter.24.cloned.1.call-start = ((), (), s32[]{:S(2)}) async-start(), calls=%async_computation.24 | async-start | bytes 12582912 | tf_op jit(solution)/shard_map/reduce_scatter | solution.py:30
  280.7 81.2 %reduce-scatter.20.cloned.1.call-start = ((), (), s32[]{:S(2)}) async-start(), calls=%async_computation.20 | async-start | bytes 25165824 | tf_op jit(solution)/shard_map/reduce_scatter | solution.py:30
  335.2 57.2 %all-gather.19.cloned.1.call-start = ((), (), s32[]{:S(2)}) async-start(), calls=%async_computation.25 | async-start | bytes 12582912 | tf_op jit(solution)/shard_map/all_gather | solution.py:26
  371.2 113.5 %reduce-scatter.26.cloned.1.call-start = ((), (), s32[]{:S(2)}) async-start(), calls=%async_computation.26 | async-start | bytes 5242880 | tf_op jit(solution)/shard_map/reduce_scatter | solution.py:22
  406.5 95.8 %copy-start.5 = (bf16[1024,256]{1,0:T(8,128)(2,1)S(1)}, bf16[1024,256]{1,0:T(8,128)(2,1)}, u32[]{:S(2)}) copy-start(bf16[1024,256]{1,0:T(8,128)(2,1)} %param.23) | copy-start | bytes 1572868
  406.6 143.4 %all-gather.21.cloned.1.call-start = ((), (), s32[]{:S(2)}) async-start(), calls=%async_computation.27 | async-start | bytes 2621440 | tf_op jit(solution)/shard_map/all_gather | solution.py:18
  504.7 57.4 %reduce-scatter.28.cloned.1.call-start = ((), (), s32[]{:S(2)}) async-start(), calls=%async_computation.28 | async-start | bytes 3145728 | tf_op jit(solution)/shard_map/reduce_scatter | solution.py:30
  554.2 95.6 %all-gather.23.cloned.1.call-start = ((), (), s32[]{:S(2)}) async-start(), calls=%async_computation.29 | async-start | bytes 4718592 | tf_op jit(solution)/shard_map/all_gather | solution.py:26
  636.2 30.4 %all-gather.15.cloned.1.call-start = ((), (), s32[]{:S(2)}) async-start(), calls=%async_computation.21 | async-start | bytes 6291456 | tf_op jit(solution)/shard_map/all_gather | solution.py:26
  636.8 109.9 %reduce-scatter.30.cloned.1.call-start = ((), (), s32[]{:S(2)}) async-start(), calls=%async_computation.30 | async-start | bytes 5242880 | tf_op jit(solution)/shard_map/reduce_scatter | solution.py:22
  658.8 168.0 %reduce-scatter.22.cloned.1.call-start = ((), (), s32[]{:S(2)}) async-start(), calls=%async_computation.22 | async-start | bytes 5242880 | tf_op jit(solution)/shard_map/reduce_scatter | solution.py:22
  676.7 240.4 %reduce-scatter.44.cloned.1.call-start = ((), (), s32[]{:S(2)}) async-start(), calls=%async_computation.37 | async-start | bytes 10485760 | tf_op jit(solution)/shard_map/reduce_scatter | solution.py:271
  687.5 268.3 %reduce-scatter.38.cloned.1.call-start = ((), (), s32[]{:S(2)}) async-start(), calls=%async_computation.34 | async-start | bytes 2621440 | tf_op jit(solution)/shard_map/reduce_scatter | solution.py:268
  692.8 352.9 %reduce-scatter.40.cloned.1.call-start = ((), (), s32[]{:S(2)}) async-start(), calls=%async_computation.35 | async-start | bytes 10485760 | tf_op jit(solution)/shard_map/reduce_scatter | solution.py:269
  703.6 432.0 %reduce-scatter.42.cloned.1.call-start = ((), (), s32[]{:S(2)}) async-start(), calls=%async_computation.36 | async-start | bytes 10485760 | tf_op jit(solution)/shard_map/reduce_scatter | solution.py:270
  714.4 460.0 %reduce-scatter.32.cloned.1.call-start = ((), (), s32[]{:S(2)}) async-start(), calls=%async_computation.31 | async-start | bytes 2621440 | tf_op jit(solution)/shard_map/reduce_scatter | solution.py:265
  719.0 494.2 %reduce-scatter.34.cloned.1.call-start = ((), (), s32[]{:S(2)}) async-start(), calls=%async_computation.32 | async-start | bytes 2621440 | tf_op jit(solution)/shard_map/reduce_scatter | solution.py:266
  723.7 23.0 %copy-start.4 = (bf16[1024,256]{1,0:T(8,128)(2,1)S(1)}, bf16[1024,256]{1,0:T(8,128)(2,1)}, u32[]{:S(2)}) copy-start(bf16[1024,256]{1,0:T(8,128)(2,1)} %param.13) | copy-start | bytes 1572868
  723.7 23.0 %copy-start.23 = (f32[1024]{0:T(1024)S(1)}, f32[1024]{0:T(1024)}, u32[]{:S(2)}) copy-start(f32[1024]{0:T(1024)} %copy-done.22) | copy-start | bytes 12292
  723.8 528.1 %reduce-scatter.36.cloned.1.call-start = ((), (), s32[]{:S(2)}) async-start(), calls=%async_computation.33 | async-start | bytes 2621440 | tf_op jit(solution)/shard_map/reduce_scatter | solution.py:267
  728.9 522.9 %copy-start.1 = (bf16[512,1024]{1,0:T(8,128)(2,1)S(1)}, bf16[512,1024]{1,0:T(8,128)(2,1)}, u32[]{:S(2)}) copy-start(bf16[512,1024]{1,0:T(8,128)(2,1)} %param.19) | copy-start | bytes 3145732
  (27 other events, 173.4 us)
Sparse Core Ops, SparseCore 0:
  29.3 44.4 all-gather.8
  83.2 12.0 reduce-scatter.15
  128.7 10.2 all-gather.10
  143.6 77.9 reduce-scatter.17
  223.1 46.9 all-gather.16
  272.1 44.4 all-gather.12
  318.8 14.4 reduce-scatter.23
  335.6 26.1 reduce-scatter.19
  371.3 21.1 all-gather.18
  406.7 77.9 reduce-scatter.25
  504.9 45.0 all-gather.20
  554.3 7.7 reduce-scatter.27
  636.3 13.3 all-gather.22
  651.7 14.8 all-gather.14
  668.7 77.9 reduce-scatter.29
  748.9 77.9 reduce-scatter.21
  830.3 86.7 reduce-scatter.43
  920.5 35.1 reduce-scatter.37
  959.4 86.3 reduce-scatter.39
  1049.2 86.3 reduce-scatter.41
  1139.1 35.1 reduce-scatter.31
  1177.9 35.1 reduce-scatter.33
  1216.7 35.1 reduce-scatter.35
where the time goes:
time: 1260 us
  waiting for transfers between devices  896 us (71%)
  matrix products  211 us (17%)
  blocking collectives  77.5 us (6%)
  other arithmetic  43.2 us (3%)
  between operations  15.5 us (1%)
    reduce_scatter x4, waiting for transfers between devices, sum_cols(): lax.psum_scatter(partial_sums, 'col', scatter_dimension=1, tiled=True)  223 us
    all_gather x4, waiting for transfers between devices, gather_cols(): return lax.all_gather(pieces, 'col', axis=1, tiled=True)  154 us
    reduce_scatter x1, waiting for transfers between devices, body(): lax.psum_scatter(grad_w_gate, 'dp', scatter_dimension=0, tiled=True)  90 us
    reduce_scatter x1, waiting for transfers between devices, body(): lax.psum_scatter(grad_w_up, 'dp', scatter_dimension=0, tiled=True)  89.8 us
    reduce_scatter x1, waiting for transfers between devices, body(): lax.psum_scatter(grad_w_down, 'dp', scatter_dimension=0, tiled=True)  87.1 us
    psum x4, blocking collectives, width_total(): return lax.psum(partial_sums, ('row', 'col'))  67.6 us
    all_gather x4, waiting for transfers between devices, gather_rows(): return lax.all_gather(pieces, 'row', axis=2, tiled=True)  51.7 us
    dot_general x7, matrix products, contract_rows(): jnp.einsum('ta,tb->ab', left, right, preferred_element_type=jnp.float32)  49.7 us
  transfers between devices with their start and end apart: 23, of which 22 were waited for; matrix products, arithmetic and copies ran while one was open for 9% of the time, Pallas kernels for 0%

commit v1 on v0

--- a/solution.py
+++ b/solution.py
@@ -1,3 +1,4 @@
+import functools
 import jax
 import jax.numpy as jnp
 from jax import lax
@@ -10,8 +11,15 @@
 masked_score = -1e30
 
 
+def roads_settle(frame, chip_axis):
+    return jnp.sum(lax.all_gather(frame, chip_axis), axis=0)
+
+
+drive_pipes = functools.partial(roads_settle, chip_axis=("row", "col"))
+
+
 def width_total(partial_sums):
-    return lax.psum(partial_sums, ("row", "col"))
+    return drive_pipes(partial_sums)
 
 
 def gather_cols(pieces):

time: 1260 us -> 1280 us (1.016)
  blocking collectives: 77.5 us -> 114 us
  waiting for transfers between devices: 896 us -> 879 us
    all_gather x0 -> x4, blocking collectives: none -> 104 us  [roads_settle(): return jnp.sum(lax.all_gather(frame, chip_axis), axis=0)]
    psum x4 -> x0, blocking collectives: 67.6 us -> none  [width_total(): return lax.psum(partial_sums, ('row', 'col'))]
where the time goes in v1:
time: 1280 us
  waiting for transfers between devices  879 us (69%)
  matrix products  211 us (16%)
  blocking collectives  114 us (9%)
  other arithmetic  43.3 us (3%)
  between operations  15.6 us (1%)
    reduce_scatter x4, waiting for transfers between devices, sum_cols(): lax.psum_scatter(partial_sums, 'col', scatter_dimension=1, tiled=True)  212 us
    all_gather x4, waiting for transfers between devices, gather_cols(): return lax.all_gather(pieces, 'col', axis=1, tiled=True)  149 us
    all_gather x4, blocking collectives, roads_settle(): return jnp.sum(lax.all_gather(frame, chip_axis), axis=0)  104 us
    reduce_scatter x1, waiting for transfers between devices, body(): lax.psum_scatter(grad_w_gate, 'dp', scatter_dimension=0, tiled=True)  90 us
    reduce_scatter x1, waiting for transfers between devices, body(): lax.psum_scatter(grad_w_up, 'dp', scatter_dimension=0, tiled=True)  89.8 us
    reduce_scatter x1, waiting for transfers between devices, body(): lax.psum_scatter(grad_w_down, 'dp', scatter_dimension=0, tiled=True)  87.1 us
    all_gather x4, waiting for transfers between devices, gather_rows(): return lax.all_gather(pieces, 'row', axis=2, tiled=True)  51.7 us
    dot_general x7, matrix products, contract_rows(): jnp.einsum('ta,tb->ab', left, right, preferred_element_type=jnp.float32)  49.7 us
  transfers between devices with their start and end apart: 23, of which 22 were waited for; matrix products, arithmetic and copies ran while one was open for 9% of the time, Pallas kernels for 0%

profile of v1, /device:TPU:0, one launch (start us, length us, event | category | flops | bytes accessed | tf_op | source)
XLA Modules:
  0.0 1278.4 jit_solution(17313869176664772305)
XLA Ops:
  8.6 25.2 %all-gather = f32[8192]{0:T(1024)S(1)} all-gather(f32[1024]{0:T(1024)S(1)} %fusion.95), channel_id=2, replica_groups=mesh['dp'=4,'row'=2,'col'=4] {'row','col'}, dimensions={0}, use_global_device_ids=true | all-gather | bytes 36864 | tf_op jit(solution)/shard_map/all_gather | solution.py:15
  36.0 47.7 %all-gather.13.cloned.1.call-done = bf16[1024,1024]{1,0:T(8,128)(2,1)} async-done(((bf16[1024,256]{1,0:T(8,128)(2,1)}), bf16[1024,1024]{1,0:T(8,128)(2,1)}) %all-gather.13.cloned.1.call-update) | async-done | bytes 2097168 | tf_op jit(solution)/shard_map/all_gather | solution.py:26
  138.5 10.4 all-gather.15.cloned.1.call-done
  154.0 77.5 %reduce-scatter.18.cloned.1.call-done = f32[1024,256]{1,0:T(8,128)} async-done(((f32[1024,1024]{1,0:T(8,128)}), f32[1024,256]{1,0:T(8,128)}) %reduce-scatter.18.cloned.1.call-update) | async-done | bytes 1048592 | tf_op jit(solution)/shard_map/reduce_scatter | solution.py:30
  232.9 27.1 %all-gather.1 = f32[8192]{0:T(1024)S(1)} all-gather(f32[1024]{0:T(1024)S(1)} %get-tuple-element.68), channel_id=3, replica_groups=mesh['dp'=4,'row'=2,'col'=4] {'row','col'}, dimensions={0}, use_global_device_ids=true | all-gather | bytes 36864 | tf_op jit(solution)/shard_map/all_gather | solution.py:15
  261.7 18.4 %all-gather.21.cloned.1.call-done = bf16[1024,1024]{1,0:T(8,128)(2,1)} async-done(((bf16[1024,256]{1,0:T(8,128)(2,1)}), bf16[1024,1024]{1,0:T(8,128)(2,1)}) %all-gather.21.cloned.1.call-update) | async-done | bytes 2097168 | tf_op jit(solution)/shard_map/all_gather | solution.py:26
  280.1 10.6 convolution_bitcast_fusion
  290.7 36.3 %all-gather.17.cloned.1.call-done = bf16[1024,1024]{1,0:T(8,128)(2,1)} async-done(((bf16[1024,256]{1,0:T(8,128)(2,1)}), bf16[1024,1024]{1,0:T(8,128)(2,1)}) %all-gather.17.cloned.1.call-update) | async-done | bytes 2097168 | tf_op jit(solution)/shard_map/all_gather | solution.py:26
  345.7 26.6 %reduce-scatter.20.cloned.1.call-done = f32[2,1024,1024]{2,1,0:T(8,128)} async-done(((f32[2,1024,2048]{2,1,0:T(8,128)}), f32[2,1024,1024]{2,1,0:T(8,128)}) %reduce-scatter.20.cloned.1.call-update) | async-done | bytes 8388624 | tf_op jit(solution)/shard_map/reduce_scatter | solution.py:38
  381.8 21.0 %all-gather.23.cloned.1.call-done = bf16[2,1024,2048]{2,1,0:T(8,128)(2,1)} async-done(((bf16[2,1024,1024]{2,1,0:T(8,128)(2,1)}), bf16[2,1024,2048]{2,1,0:T(8,128)(2,1)}) %all-gather.23.cloned.1.call-update) | async-done | bytes 8388624 | tf_op jit(solution)/shard_map/all_gather | solution.py:34
  417.1 78.1 %reduce-scatter.26.cloned.1.call-done = f32[1024,256]{1,0:T(8,128)} async-done(((f32[1024,1024]{1,0:T(8,128)}), f32[1024,256]{1,0:T(8,128)}) %reduce-scatter.26.cloned.1.call-update) | async-done | bytes 1048592 | tf_op jit(solution)/shard_map/reduce_scatter | solution.py:30
  496.8 24.1 %all-gather.2 = f32[8192]{0:T(1024)S(1)} all-gather(f32[1024]{0:T(1024)S(1)} %get-tuple-element.53), channel_id=4, replica_groups=mesh['dp'=4,'row'=2,'col'=4] {'row','col'}, dimensions={0}, use_global_device_ids=true | all-gather | bytes 36864 | tf_op jit(solution)/shard_map/all_gather | solution.py:15
  523.4 46.5 %all-gather.25.cloned.1.call-done = bf16[1024,1024]{1,0:T(8,128)(2,1)} async-done(((bf16[1024,256]{1,0:T(8,128)(2,1)}), bf16[1024,1024]{1,0:T(8,128)(2,1)}) %all-gather.25.cloned.1.call-update) | async-done | bytes 2097168 | tf_op jit(solution)/shard_map/all_gather | solution.py:26
  588.1 12.7 fusion.29
  600.7 13.5 %fusion.74 = f32[512,4,64]{0,2,1:T(8,128)} fusion(f32[4,512,1024]{2,1,0:T(8,128)} %fusion.5, f32[4,512,1024]{2,1,0:T(8,128)} %fusion.132, bf16[1024,4,32]{0,2,1:T(8,128)(2,1)} %get-tuple-element.80, bf16[1024,4,32]{0,2,1:T(8,128)(2,1)S(1)} %copy-done.20), kind=kOutput, calls=%fused_computation.81 | convolution fusion | flops 279972864 | bytes 17825792 | tf_op jit(solution)/shard_map/while/body/eval_jaxpr/hqk,khd->qhd/dot_general | solution.py:149
  623.9 12.0 fusion.71
  636.0 14.0 %fusion.65 = f32[1024,4,64]{0,2,1:T(8,128)} fusion(f32[4,64,1024]{2,1,0:T(8,128)} %fusion.29, f32[4,512,1024]{2,1,0:T(8,128)} %fusion.4, f32[4,512,1024]{2,1,0:T(8,128)} %fusion.133, bf16[1024,4,32]{0,2,1:T(8,128)(2,1)} %get-tuple-element.89, bf16[1024,4,32]{0,2,1:T(8,128)(2,1)} %get-tuple-element.90), kind=kOutput, calls=%fused_computation.78 | convolution fusion | flops 279710720 | bytes 19398656 | tf_op jit(solution)/shard_map/while/body/eval_jaxpr/hqk,qhd->khd/dot_general | solution.py:151
  657.2 12.5 all-gather.27.cloned.1.call-done
  686.6 10.1 fusion.20
  696.8 10.7 fusion.18
  712.9 10.6 fusion.40
  723.6 10.7 fusion.42
  749.7 17.1 %reduce-scatter.30.cloned.1.call-done = f32[1024,256]{1,0:T(8,128)} async-done(((f32[1024,1024]{1,0:T(8,128)}), f32[1024,256]{1,0:T(8,128)}) %reduce-scatter.30.cloned.1.call-update) | async-done | bytes 1048592 | tf_op jit(solution)/shard_map/reduce_scatter | solution.py:30
  768.5 27.7 %all-gather.3 = f32[8192]{0:T(1024)S(1)} all-gather(f32[1024]{0:T(1024)S(1)} %get-tuple-element.55), channel_id=5, replica_groups=mesh['dp'=4,'row'=2,'col'=4] {'row','col'}, dimensions={0}, use_global_device_ids=true | all-gather | bytes 36864 | tf_op jit(solution)/shard_map/all_gather | solution.py:15
  807.2 39.5 %reduce-scatter.22.cloned.1.call-done = f32[1024,256]{1,0:T(8,128)} async-done(((f32[1024,1024]{1,0:T(8,128)}), f32[1024,256]{1,0:T(8,128)}) %reduce-scatter.22.cloned.1.call-update) | async-done | bytes 1048592 | tf_op jit(solution)/shard_map/reduce_scatter | solution.py:30
  849.8 87.1 %reduce-scatter.44.cloned.1.call-done = f32[512,1024]{1,0:T(8,128)} async-done(((f32[2048,1024]{1,0:T(8,128)}), f32[512,1024]{1,0:T(8,128)}) %reduce-scatter.44.cloned.1.call-update) | async-done | bytes 2097168 | tf_op jit(solution)/shard_map/reduce_scatter | solution.py:279
  936.9 38.6 %reduce-scatter.38.cloned.1.call-done = f32[128,1024]{1,0:T(8,128)} async-done(((f32[512,1024]{1,0:T(8,128)}), f32[128,1024]{1,0:T(8,128)}) %reduce-scatter.38.cloned.1.call-update) | async-done | bytes 524304 | tf_op jit(solution)/shard_map/reduce_scatter | solution.py:276
  975.5 90.0 %reduce-scatter.40.cloned.1.call-done = f32[256,2048]{1,0:T(8,128)} async-done(((f32[1024,2048]{1,0:T(8,128)}), f32[256,2048]{1,0:T(8,128)}) %reduce-scatter.40.cloned.1.call-update) | async-done | bytes 2097168 | tf_op jit(solution)/shard_map/reduce_scatter | solution.py:277
  1065.5 89.8 %reduce-scatter.42.cloned.1.call-done = f32[256,2048]{1,0:T(8,128)} async-done(((f32[1024,2048]{1,0:T(8,128)}), f32[256,2048]{1,0:T(8,128)}) %reduce-scatter.42.cloned.1.call-update) | async-done | bytes 2097168 | tf_op jit(solution)/shard_map/reduce_scatter | solution.py:278
  1155.3 38.8 %reduce-scatter.32.cloned.1.call-done = f32[256,512]{1,0:T(8,128)} async-done(((f32[1024,512]{1,0:T(8,128)}), f32[256,512]{1,0:T(8,128)}) %reduce-scatter.32.cloned.1.call-update) | async-done | bytes 524304 | tf_op jit(solution)/shard_map/reduce_scatter | solution.py:273
  1194.1 38.8 %reduce-scatter.34.cloned.1.call-done = f32[256,512]{1,0:T(8,128)} async-done(((f32[1024,512]{1,0:T(8,128)}), f32[256,512]{1,0:T(8,128)}) %reduce-scatter.34.cloned.1.call-update) | async-done | bytes 524304 | tf_op jit(solution)/shard_map/reduce_scatter | solution.py:274
  1232.9 38.8 %reduce-scatter.36.cloned.1.call-done = f32[256,512]{1,0:T(8,128)} async-done(((f32[1024,512]{1,0:T(8,128)}), f32[256,512]{1,0:T(8,128)}) %reduce-scatter.36.cloned.1.call-update) | async-done | bytes 524304 | tf_op jit(solution)/shard_map/reduce_scatter | solution.py:275
  (194 shorter events, 200.4 us)
Async XLA Ops:
  7.2 141.7 %copy-start = (bf16[512,1024]{1,0:T(8,128)(2,1)S(1)}, bf16[512,1024]{1,0:T(8,128)(2,1)}, u32[]{:S(2)}) copy-start(bf16[512,1024]{1,0:T(8,128)(2,1)} %param.19) | copy-start | bytes 3145732
  7.2 76.5 %all-gather.13.cloned.1.call-start = ((), (), s32[]{:S(2)}) async-start(), calls=%async_computation.15 | async-start | bytes 2621440 | tf_op jit(solution)/shard_map/all_gather | solution.py:26
  33.9 53.1 %copy-start.22 = (f32[1024]{0:T(1024)}, f32[1024]{0:T(1024)S(1)}, u32[]{:S(2)}) copy-start(f32[1024]{0:T(1024)S(1)} %add_rsqrt_fusion.1) | copy-start | bytes 12292
  35.9 51.1 %copy-start.34 = (bf16[1024,512]{1,0:T(8,128)(2,1)S(1)}, bf16[1024,512]{1,0:T(8,128)(2,1)}, u32[]{:S(2)}) copy-start(bf16[1024,512]{1,0:T(8,128)(2,1)} %param.17) | copy-start | bytes 3145732
  36.0 69.1 %reduce-scatter.16.cloned.1.call-start = ((), (), s32[]{:S(2)}) async-start(), calls=%async_computation.16 | async-start | bytes 9437184 | tf_op jit(solution)/shard_map/reduce_scatter | solution.py:38
  92.9 56.0 %all-gather.15.cloned.1.call-start = ((), (), s32[]{:S(2)}) async-start(), calls=%async_computation.17 | async-start | bytes 1572864 | tf_op jit(solution)/shard_map/all_gather | solution.py:34
  138.4 93.1 %reduce-scatter.18.cloned.1.call-start = ((), (), s32[]{:S(2)}) async-start(), calls=%async_computation.18 | async-start | bytes 5242880 | tf_op jit(solution)/shard_map/reduce_scatter | solution.py:30
  153.3 78.2 %copy-start.3 = (bf16[1024,256]{1,0:T(8,128)(2,1)S(1)}, bf16[1024,256]{1,0:T(8,128)(2,1)}, u32[]{:S(2)}) copy-start(bf16[1024,256]{1,0:T(8,128)(2,1)} %param.13) | copy-start | bytes 1572868
  153.3 106.7 %copy-start.24 = (f32[256]{0:T(256)S(1)}, f32[256]{0:T(256)}, u32[]{:S(2)}) copy-start(f32[256]{0:T(256)} %param.15) | copy-start | bytes 3076
  153.4 126.7 %all-gather.21.cloned.1.call-start = ((), (), s32[]{:S(2)}) async-start(), calls=%async_computation.23 | async-start | bytes 2621440 | tf_op jit(solution)/shard_map/all_gather | solution.py:26
  154.0 173.0 %all-gather.17.cloned.1.call-start = ((), (), s32[]{:S(2)}) async-start(), calls=%async_computation.19 | async-start | bytes 2621440 | tf_op jit(solution)/shard_map/all_gather | solution.py:26
  261.1 84.6 %reduce-scatter.24.cloned.1.call-start = ((), (), s32[]{:S(2)}) async-start(), calls=%async_computation.24 | async-start | bytes 12582912 | tf_op jit(solution)/shard_map/reduce_scatter | solution.py:38
  290.7 81.6 %reduce-scatter.20.cloned.1.call-start = ((), (), s32[]{:S(2)}) async-start(), calls=%async_computation.20 | async-start | bytes 25165824 | tf_op jit(solution)/shard_map/reduce_scatter | solution.py:38
  345.6 57.3 %all-gather.23.cloned.1.call-start = ((), (), s32[]{:S(2)}) async-start(), calls=%async_computation.25 | async-start | bytes 12582912 | tf_op jit(solution)/shard_map/all_gather | solution.py:34
  381.6 113.5 %reduce-scatter.26.cloned.1.call-start = ((), (), s32[]{:S(2)}) async-start(), calls=%async_computation.26 | async-start | bytes 5242880 | tf_op jit(solution)/shard_map/reduce_scatter | solution.py:30
  417.0 103.9 %copy-start.5 = (bf16[1024,256]{1,0:T(8,128)(2,1)S(1)}, bf16[1024,256]{1,0:T(8,128)(2,1)}, u32[]{:S(2)}) copy-start(bf16[1024,256]{1,0:T(8,128)(2,1)} %param.23) | copy-start | bytes 1572868
  417.0 152.9 %all-gather.25.cloned.1.call-start = ((), (), s32[]{:S(2)}) async-start(), calls=%async_computation.27 | async-start | bytes 2621440 | tf_op jit(solution)/shard_map/all_gather | solution.py:26
  523.3 58.7 %reduce-scatter.28.cloned.1.call-start = ((), (), s32[]{:S(2)}) async-start(), calls=%async_computation.28 | async-start | bytes 3145728 | tf_op jit(solution)/shard_map/reduce_scatter | solution.py:38
  574.1 95.6 %all-gather.27.cloned.1.call-start = ((), (), s32[]{:S(2)}) async-start(), calls=%async_computation.29 | async-start | bytes 4718592 | tf_op jit(solution)/shard_map/all_gather | solution.py:34
  656.2 30.4 %all-gather.19.cloned.1.call-start = ((), (), s32[]{:S(2)}) async-start(), calls=%async_computation.21 | async-start | bytes 6291456 | tf_op jit(solution)/shard_map/all_gather | solution.py:34
  656.7 110.0 %reduce-scatter.30.cloned.1.call-start = ((), (), s32[]{:S(2)}) async-start(), calls=%async_computation.30 | async-start | bytes 5242880 | tf_op jit(solution)/shard_map/reduce_scatter | solution.py:30
  678.8 167.9 %reduce-scatter.22.cloned.1.call-start = ((), (), s32[]{:S(2)}) async-start(), calls=%async_computation.22 | async-start | bytes 5242880 | tf_op jit(solution)/shard_map/reduce_scatter | solution.py:30
  696.7 240.2 %reduce-scatter.44.cloned.1.call-start = ((), (), s32[]{:S(2)}) async-start(), calls=%async_computation.37 | async-start | bytes 10485760 | tf_op jit(solution)/shard_map/reduce_scatter | solution.py:279
  707.5 268.1 %reduce-scatter.38.cloned.1.call-start = ((), (), s32[]{:S(2)}) async-start(), calls=%async_computation.34 | async-start | bytes 2621440 | tf_op jit(solution)/shard_map/reduce_scatter | solution.py:276
  712.8 352.7 %reduce-scatter.40.cloned.1.call-start = ((), (), s32[]{:S(2)}) async-start(), calls=%async_computation.35 | async-start | bytes 10485760 | tf_op jit(solution)/shard_map/reduce_scatter | solution.py:277
  723.5 431.8 %reduce-scatter.42.cloned.1.call-start = ((), (), s32[]{:S(2)}) async-start(), calls=%async_computation.36 | async-start | bytes 10485760 | tf_op jit(solution)/shard_map/reduce_scatter | solution.py:278
  734.3 459.8 %reduce-scatter.32.cloned.1.call-start = ((), (), s32[]{:S(2)}) async-start(), calls=%async_computation.31 | async-start | bytes 2621440 | tf_op jit(solution)/shard_map/reduce_scatter | solution.py:273
  738.9 494.0 %reduce-scatter.34.cloned.1.call-start = ((), (), s32[]{:S(2)}) async-start(), calls=%async_computation.32 | async-start | bytes 2621440 | tf_op jit(solution)/shard_map/reduce_scatter | solution.py:274
  743.7 23.0 %copy-start.4 = (bf16[1024,256]{1,0:T(8,128)(2,1)S(1)}, bf16[1024,256]{1,0:T(8,128)(2,1)}, u32[]{:S(2)}) copy-start(bf16[1024,256]{1,0:T(8,128)(2,1)} %param.13) | copy-start | bytes 1572868
  743.7 23.0 %copy-start.23 = (f32[1024]{0:T(1024)S(1)}, f32[1024]{0:T(1024)}, u32[]{:S(2)}) copy-start(f32[1024]{0:T(1024)} %copy-done.22) | copy-start | bytes 12292
  743.7 527.9 %reduce-scatter.36.cloned.1.call-start = ((), (), s32[]{:S(2)}) async-start(), calls=%async_computation.33 | async-start | bytes 2621440 | tf_op jit(solution)/shard_map/reduce_scatter | solution.py:275
  748.9 522.7 %copy-start.1 = (bf16[512,1024]{1,0:T(8,128)(2,1)S(1)}, bf16[512,1024]{1,0:T(8,128)(2,1)}, u32[]{:S(2)}) copy-start(bf16[512,1024]{1,0:T(8,128)(2,1)} %param.19) | copy-start | bytes 3145732
  (27 other events, 173.4 us)
Sparse Core Ops, SparseCore 0:
  36.1 47.6 all-gather.12
  93.0 11.9 reduce-scatter.15
  138.5 10.3 all-gather.14
  153.5 77.9 reduce-scatter.17
  232.9 47.0 all-gather.20
  282.0 44.8 all-gather.16
  329.2 14.4 reduce-scatter.23
  346.0 26.2 reduce-scatter.19
  381.7 21.1 all-gather.22
  417.1 77.9 reduce-scatter.25
  523.5 46.4 all-gather.24
  574.2 7.7 reduce-scatter.27
  656.3 13.3 all-gather.26
  671.7 14.8 all-gather.18
  688.7 77.9 reduce-scatter.29
  768.9 77.7 reduce-scatter.21
  850.2 86.6 reduce-scatter.43
  940.3 35.1 reduce-scatter.37
  979.2 86.3 reduce-scatter.39
  1069.0 86.3 reduce-scatter.41
  1158.9 35.1 reduce-scatter.31
  1197.7 35.1 reduce-scatter.33
  1236.4 35.1 reduce-scatter.35
